TPU v7x, 32 devices: a whole 2x2x4 slice. The times are simulated.
32 devices in a mesh: dom: 32 (over z, y, x, core).
Axes of the slice: x: 2, y: 2, z: 4, core: 2. Of those that a mesh axis runs over, the one named last changes fastest.
Arguments:
- right_side: float32 [18, 32768], P(None, 'dom'), may hold values from -20 to 20
- element_matrix: bfloat16 [72, 72, 16384], P(None, None, 'dom'), may hold values from -8 to 8, as said below
- face_map: int32 [4, 16384], P(None, 'dom'), may hold values from 0 to 1535
- share_index: int32 [32, 4, 128], P('dom'), may hold values from 0 to 1023
- share_count: int32 [32, 4], P('dom'), may hold values from 0 to 128, as said below
- face_mass: float32 [32768], P('dom'), may hold values from 0.5 to 2
- absorbing: int32 [32768], P('dom'), may hold values 0 or 1
- impedance: float32 [32768], P('dom'), may hold values from 0.5 to 4
Outputs:
- solution: float32 [18, 32768], P(None, 'dom')
- residual: float32 [18, 32768], P(None, 'dom')
Inputs may be any that keep to these rules, and one draw needn't show every extreme that they name: `element_matrix`: each element's 72 x 72 matrix is symmetric positive definite. share_count[d, k] is 0 where device d + o_k lies outside the axis; it equals 128 for some device and offset in every draw.
All inputs are finite; a program needn't handle non-finite values. No bound on the sum of `absorbing` on one device may be relied on, other than what follows from the above.
Results may differ from a plain program's by a relative error of at most 0.0003.
Values sent between devices are 32-bit elements; how exact they have to be, the bound alone decides.
A program may use at most 64 MiB of HBM per device.

v0:
```python
import jax
import jax.numpy as jnp
from jax import lax
from jax.sharding import PartitionSpec as P

ITERS = 2


def passed_along(value, axis, steps):
    count = lax.axis_size(axis)
    first, last = (max(0, -steps), min(count, count - steps))
    return lax.ppermute(value, axis, [(source, source + steps) for source in range(first, last)])


def offset_list(block_count):
    half_count = block_count // 2
    return [
        block_index - half_count if block_index < half_count else block_index - half_count + 1
        for block_index in range(block_count)
    ]


def shards(
    right_side, element_matrix, face_map, share_index, share_count, face_mass, absorbing, impedance
):
    trace_width = right_side.shape[0]
    own_faces = right_side.shape[1]
    side_count = face_map.shape[0]
    element_count = face_map.shape[1]
    block_count = share_index.shape[1]
    block_width = share_index.shape[2]
    dof_count = side_count * trace_width
    slot_total = own_faces + block_count * block_width
    offsets = offset_list(block_count)
    send_rows = share_index[0]
    slot_iota = lax.broadcasted_iota(jnp.int32, (block_count, block_width), 1)
    alive_mask = (slot_iota < share_count[0][:, None]).astype(jnp.float32)
    diagonal = face_mass + absorbing.astype(jnp.float32) * impedance
    flat_map = face_map.reshape(side_count * element_count)
    selector = (
        lax.broadcasted_iota(jnp.int32, (slot_total, side_count * element_count), 0)
        == flat_map[None, :]
    ).astype(jnp.float32)

    def fetch_ghosts(outgoing):
        received = []
        for block_index in range(block_count):
            received.append(passed_along(outgoing[block_index], "dom", offsets[block_index]))
        return jnp.stack(received)

    def return_sums(partial_value):
        received = []
        for block_index in range(block_count):
            received.append(passed_along(partial_value[block_index], "dom", -offsets[block_index]))
        return jnp.stack(received)

    def operate(field_now):
        outgoing = (
            jnp.take(field_now, send_rows, axis=1).transpose(1, 0, 2) * alive_mask[:, None, :]
        )
        ghosts = fetch_ghosts(outgoing)
        extended = jnp.concatenate(
            [field_now, ghosts.transpose(1, 0, 2).reshape(trace_width, block_count * block_width)],
            axis=1,
        )
        gathered = jnp.dot(
            extended, selector, precision=lax.Precision.HIGHEST, preferred_element_type=jnp.float32
        )
        picked = (
            gathered.reshape(trace_width, side_count, element_count)
            .transpose(1, 0, 2)
            .reshape(dof_count, element_count)
        )
        product = jnp.sum(element_matrix.astype(jnp.float32) * picked[None, :, :], axis=1)
        spread = (
            product.reshape(side_count, trace_width, element_count)
            .transpose(1, 0, 2)
            .reshape(trace_width, side_count * element_count)
        )
        summed = lax.dot_general(
            spread,
            selector,
            (((1,), (1,)), ((), ())),
            precision=lax.Precision.HIGHEST,
            preferred_element_type=jnp.float32,
        )
        partial_value = (
            summed[:, own_faces:].reshape(trace_width, block_count, block_width).transpose(1, 0, 2)
        )
        returned = return_sums(partial_value) * alive_mask[:, None, :]
        result = summed[:, :own_faces].at[:, send_rows].add(returned.transpose(1, 0, 2))
        return result + diagonal[None, :] * field_now

    def paired(values, image_vec):
        return lax.psum((jnp.sum(values * values), jnp.sum(values * image_vec)), "dom")

    solution = jnp.zeros_like(right_side)
    residual = right_side
    image_vec = operate(residual)
    norm_now, curvature = paired(residual, image_vec)
    step_size = norm_now / curvature
    direction = residual
    image_dir = image_vec
    for rounds in range(ITERS):
        solution = solution + step_size * direction
        residual = residual - step_size * image_dir
        if rounds + 1 < ITERS:
            image_vec = operate(residual)
            norm_next, curvature = paired(residual, image_vec)
            beta_ratio = norm_next / norm_now
            step_size = norm_next / (curvature - beta_ratio * norm_next / step_size)
            direction = residual + beta_ratio * direction
            image_dir = image_vec + beta_ratio * image_dir
            norm_now = norm_next
    return (solution, residual)


def solution(mesh):
    placed = (
        P(None, "dom"),
        P(None, None, "dom"),
        P(None, "dom"),
        P("dom", None, None),
        P("dom", None),
        P("dom"),
        P("dom"),
        P("dom"),
    )
    return jax.shard_map(
        shards,
        mesh=mesh,
        in_specs=placed,
        out_specs=(P(None, "dom"), P(None, "dom")),
        check_vma=False,
    )
```

profile of v0, /device:TPU:0, one launch (start us, length us, event | category | flops | bytes accessed | tf_op | source)
XLA Modules:
  0.0 199.9 jit_solution(12577031938445151586)
XLA Ops:
  0.6 0.7 fusion.22
  1.3 0.8 fusion.21
  2.1 1.1 copy.41
  3.2 1.0 gather_fusion
  4.4 1.3 collective-permute-start
  5.7 5.5 %collective-permute-start.3 = (f32[18,128]{1,0:T(8,128)S(1)}, f32[18,128]{1,0:T(8,128)S(1)}, u32[]{:S(2)}, u32[]{:S(2)}) collective-permute-start(f32[18,128]{1,0:T(8,128)S(1)} %get-tuple-element.22), channel_id=1, source_target_pairs={{0,2},{1,3},{2,4},{3,5},{4,6},{5,7},{6,8},{7,9},{8,10},{9,11},{10,... | collective-permute-start | bytes 27656 | tf_op jit(solution)/shard_map/ppermute | solution.py:12
  11.2 1.5 collective-permute-start.2
  12.7 1.3 collective-permute-start.1
  14.0 0.7 multiply_add_fusion.1
  14.7 0.7 fusion.20
  15.4 0.7 copy.61
  16.1 2.6 %collective-permute-done.1 = f32[18,128]{1,0:T(8,128)S(1)} collective-permute-done((f32[18,128]{1,0:T(8,128)S(1)}, f32[18,128]{1,0:T(8,128)S(1)}, u32[]{:S(2)}, u32[]{:S(2)}) %collective-permute-start.1) | collective-permute-done | bytes 9248 | tf_op jit(solution)/shard_map/ppermute | solution.py:12
  18.8 4.9 %fusion.3 = f32[18,2048]{1,0:T(8,128)S(1)} fusion(s32[2048]{0:T(1024)S(1)} %bitcast.155, f32[18,512]{1,0:T(8,128)S(1)} %bitcast.133, f32[18,1024]{1,0:T(8,128)} %param.10), kind=kOutput, calls=%fused_computation.10 | convolution fusion | flops 682650624 | bytes 266240 | tf_op jit(solution)/shard_map/dot_general | solution.py:66
  23.9 4.1 %fusion.4 = f32[72,512]{1,0:T(8,128)S(1)} fusion(bf16[72,72,512]{2,1,0:T(8,128)(2,1)} %param.11, f32[72,512]{1,0:T(8,128)S(1)} %mul.120), kind=kLoop, calls=%fused_computation.11 | loop fusion | flops 7925760 | bytes 5603328 | tf_op jit(solution)/shard_map/reduce_sum | solution.py:74
  28.2 5.6 %fusion.2 = f32[18,1536]{1,0:T(8,128)S(1)} fusion(f32[18,2048]{1,0:T(8,128)S(1)} %bitcast.128, s32[2048]{0:T(1024)S(1)} %bitcast.156), kind=kOutput, calls=%fused_computation.9 | convolution fusion | flops 682622976 | bytes 266240 | tf_op jit(solution)/shard_map/dot_general | solution.py:80
  34.0 1.3 collective-permute-start.6
  35.3 1.3 collective-permute-start.7
  36.6 5.0 %collective-permute-start.5 = (f32[18,128]{1,0:T(8,128)S(1)}, f32[18,128]{1,0:T(8,128)S(1)}, u32[]{:S(2)}, u32[]{:S(2)}) collective-permute-start(f32[18,128]{1,0:T(8,128)S(1)} %bitcast.148), channel_id=1, source_target_pairs={{0,1},{1,2},{2,3},{3,4},{4,5},{5,6},{6,7},{7,8},{8,9},{9,10},{10,1... | collective-permute-start | bytes 27656 | tf_op jit(solution)/shard_map/ppermute | solution.py:12
  41.5 4.3 %collective-permute-start.4 = (f32[18,128]{1,0:T(8,128)S(1)}, f32[18,128]{1,0:T(8,128)S(1)}, u32[]{:S(2)}, u32[]{:S(2)}) collective-permute-start(f32[18,128]{1,0:T(8,128)S(1)} %bitcast.147), channel_id=1, source_target_pairs={{0,2},{1,3},{2,4},{3,5},{4,6},{5,7},{6,8},{7,9},{8,10},{9,11},{10,... | collective-permute-start | bytes 27656 | tf_op jit(solution)/shard_map/ppermute | solution.py:12
  45.8 0.6 multiply_reduce_fusion.3
  46.5 0.2 copy.40
  46.7 0.5 collective-permute-done.4
  47.2 0.1 copy.39
  47.4 3.7 %scatter_fusion = f32[18,1024]{0,1:T(8,128)S(1)} fusion(f32[18,1024]{0,1:T(8,128)S(1)} %copy.40, s32[512]{0:T(512)S(1)} %fusion.20, f32[512,18]{1,0:T(8,128)S(1)} %bitcast.124), kind=kCustom, calls=%fused_computation.2 | custom fusion | flops 9216 | bytes 112640 | tf_op jit(solution)/shard_map/scatter-add | solution.py:91
  51.1 0.7 multiply_reduce_fusion
  51.8 0.2 copy.42
  52.0 45.5 %all-reduce.1 = (f32[]{:T(128)}, f32[]{:T(128)}) all-reduce(f32[]{:T(128)} %get-tuple-element.11, f32[]{:T(128)} %multiply_reduce_fusion), channel_id=1, replica_groups=mesh['dom'=32] {'dom'}, use_global_device_ids=true, to_apply=%region_1.2 | all-reduce | flops 2 | bytes 16 | tf_op jit(solution)/shard_map/psum | solution.py:95
  98.9 0.2 copy.43
  99.1 1.0 gather_fusion.1
  100.3 1.3 collective-permute-start.8
  101.6 1.3 collective-permute-start.10
  102.9 1.3 collective-permute-start.9
  104.2 7.8 %collective-permute-start.11 = (f32[18,128]{1,0:T(8,128)S(1)}, f32[18,128]{1,0:T(8,128)S(1)}, u32[]{:S(2)}, u32[]{:S(2)}) collective-permute-start(f32[18,128]{1,0:T(8,128)S(1)} %get-tuple-element.18), channel_id=1, source_target_pairs={{0,2},{1,3},{2,4},{3,5},{4,6},{5,7},{6,8},{7,9},{8,10},{9,11},{10,... | collective-permute-start | bytes 27656 | tf_op jit(solution)/shard_map/ppermute | solution.py:12
  112.1 1.3 collective-permute-done.11
  113.4 4.0 %fusion.1 = f32[18,2048]{1,0:T(8,128)S(1)} fusion(s32[2048]{0:T(1024)S(1)} %bitcast.157, f32[18,512]{1,0:T(8,128)S(1)} %bitcast.134, f32[18,1024]{1,0:T(8,128)S(1)} %multiply_subtract_fusion.1), kind=kOutput, calls=%fused_computation.8 | convolution fusion | flops 682650624 | bytes 266240 | tf_op jit(solution)/shard_map/dot_general | solution.py:66
  117.7 4.0 %fusion.5 = f32[72,512]{1,0:T(8,128)S(1)} fusion(bf16[72,72,512]{2,1,0:T(8,128)(2,1)} %param.11, f32[72,512]{1,0:T(8,128)S(1)} %mul.135), kind=kLoop, calls=%fused_computation.12 | loop fusion | flops 7925760 | bytes 5603328 | tf_op jit(solution)/shard_map/reduce_sum | solution.py:74
  122.0 5.6 %fusion = f32[18,1536]{1,0:T(8,128)S(1)} fusion(f32[18,2048]{1,0:T(8,128)S(1)} %bitcast.127, s32[2048]{0:T(1024)S(1)} %bitcast.158), kind=kOutput, calls=%fused_computation.7 | convolution fusion | flops 682622976 | bytes 266240 | tf_op jit(solution)/shard_map/dot_general | solution.py:80
  127.7 5.7 %collective-permute-start.12 = (f32[18,128]{1,0:T(8,128)S(1)}, f32[18,128]{1,0:T(8,128)S(1)}, u32[]{:S(2)}, u32[]{:S(2)}) collective-permute-start(f32[18,128]{1,0:T(8,128)S(1)} %get-tuple-element.13), channel_id=1, source_target_pairs={{0,2},{1,3},{2,4},{3,5},{4,6},{5,7},{6,8},{7,9},{8,10},{9,11},{10,... | collective-permute-start | bytes 27656 | tf_op jit(solution)/shard_map/ppermute | solution.py:12
  133.4 1.3 collective-permute-start.15
  134.7 1.3 collective-permute-start.14
  136.0 3.0 %collective-permute-start.13 = (f32[18,128]{1,0:T(8,128)S(1)}, f32[18,128]{1,0:T(8,128)S(1)}, u32[]{:S(2)}, u32[]{:S(2)}) collective-permute-start(f32[18,128]{1,0:T(8,128)S(1)} %get-tuple-element.16), channel_id=1, source_target_pairs={{0,1},{1,2},{2,3},{3,4},{4,5},{5,6},{6,7},{7,8},{8,9},{9,10},{10,1... | collective-permute-start | bytes 27656 | tf_op jit(solution)/shard_map/ppermute | solution.py:12
  139.0 0.2 copy.52
  139.3 0.9 collective-permute-done.15
  140.3 3.7 %scatter_fusion.1 = f32[18,1024]{0,1:T(8,128)S(1)} fusion(f32[18,1024]{0,1:T(8,128)S(1)} %copy.52, s32[512]{0:T(512)S(1)} %fusion.20, f32[512,18]{1,0:T(8,128)S(1)} %bitcast.123), kind=kCustom, calls=%fused_computation.3 | custom fusion | flops 9216 | bytes 112640 | tf_op jit(solution)/shard_map/scatter-add | solution.py:91
  144.0 0.2 copy.53
  144.2 0.7 multiply_reduce_fusion.1
  145.0 49.7 %all-reduce = (f32[]{:T(128)}, f32[]{:T(128)}) all-reduce(f32[]{:T(128)} %get-tuple-element.4, f32[]{:T(128)} %get-tuple-element.3), channel_id=1, replica_groups=mesh['dom'=32] {'dom'}, use_global_device_ids=true, to_apply=%region_7.9 | all-reduce | flops 2 | bytes 16 | tf_op jit(solution)/shard_map/psum | solution.py:95
  199.2 0.7 multiply_subtract_fusion
  (62 shorter events, 1.5 us)
Async XLA Ops:
  4.4 11.7 %collective-permute-start = (f32[18,128]{1,0:T(8,128)S(1)}, f32[18,128]{1,0:T(8,128)S(1)}, u32[]{:S(2)}, u32[]{:S(2)}) collective-permute-start(f32[18,128]{1,0:T(8,128)S(1)} %get-tuple-element.21), channel_id=1, source_target_pairs={{2,0},{3,1},{4,2},{5,3},{6,4},{7,5},{8,6},{9,7},{10,8},{11,9},{12,... | collective-permute-start | bytes 27656 | tf_op jit(solution)/shard_map/ppermute | solution.py:12
  5.7 10.4 %collective-permute-start.3 = (f32[18,128]{1,0:T(8,128)S(1)}, f32[18,128]{1,0:T(8,128)S(1)}, u32[]{:S(2)}, u32[]{:S(2)}) collective-permute-start(f32[18,128]{1,0:T(8,128)S(1)} %get-tuple-element.22), channel_id=1, source_target_pairs={{0,2},{1,3},{2,4},{3,5},{4,6},{5,7},{6,8},{7,9},{8,10},{9,11},{10,... | collective-permute-start | bytes 27656 | tf_op jit(solution)/shard_map/ppermute | solution.py:12
  11.2 4.9 %collective-permute-start.2 = (f32[18,128]{1,0:T(8,128)S(1)}, f32[18,128]{1,0:T(8,128)S(1)}, u32[]{:S(2)}, u32[]{:S(2)}) collective-permute-start(f32[18,128]{1,0:T(8,128)S(1)} %get-tuple-element.23), channel_id=1, source_target_pairs={{0,1},{1,2},{2,3},{3,4},{4,5},{5,6},{6,7},{7,8},{8,9},{9,10},{10,1... | collective-permute-start | bytes 27656 | tf_op jit(solution)/shard_map/ppermute | solution.py:12
  12.7 6.1 %collective-permute-start.1 = (f32[18,128]{1,0:T(8,128)S(1)}, f32[18,128]{1,0:T(8,128)S(1)}, u32[]{:S(2)}, u32[]{:S(2)}) collective-permute-start(f32[18,128]{1,0:T(8,128)S(1)} %get-tuple-element.24), channel_id=1, source_target_pairs={{1,0},{2,1},{3,2},{4,3},{5,4},{6,5},{7,6},{8,7},{9,8},{10,9},{11,1... | collective-permute-start | bytes 27656 | tf_op jit(solution)/shard_map/ppermute | solution.py:12
  23.9 21.9 %copy-start = (f32[18,1024]{1,0:T(8,128)S(1)}, f32[18,1024]{1,0:T(8,128)}, u32[]{:S(2)}) copy-start(f32[18,1024]{1,0:T(8,128)} %param.10) | copy-start | bytes 221188
  34.0 12.7 %collective-permute-start.6 = (f32[18,128]{1,0:T(8,128)S(1)}, f32[18,128]{1,0:T(8,128)S(1)}, u32[]{:S(2)}, u32[]{:S(2)}) collective-permute-start(f32[18,128]{1,0:T(8,128)S(1)} %bitcast.150), channel_id=1, source_target_pairs={{1,0},{2,1},{3,2},{4,3},{5,4},{6,5},{7,6},{8,7},{9,8},{10,9},{11,1... | collective-permute-start | bytes 27656 | tf_op jit(solution)/shard_map/ppermute | solution.py:12
  35.3 11.4 %collective-permute-start.7 = (f32[18,128]{1,0:T(8,128)S(1)}, f32[18,128]{1,0:T(8,128)S(1)}, u32[]{:S(2)}, u32[]{:S(2)}) collective-permute-start(f32[18,128]{1,0:T(8,128)S(1)} %bitcast.149), channel_id=1, source_target_pairs={{2,0},{3,1},{4,2},{5,3},{6,4},{7,5},{8,6},{9,7},{10,8},{11,9},{12,... | collective-permute-start | bytes 27656 | tf_op jit(solution)/shard_map/ppermute | solution.py:12
  36.6 10.1 %collective-permute-start.5 = (f32[18,128]{1,0:T(8,128)S(1)}, f32[18,128]{1,0:T(8,128)S(1)}, u32[]{:S(2)}, u32[]{:S(2)}) collective-permute-start(f32[18,128]{1,0:T(8,128)S(1)} %bitcast.148), channel_id=1, source_target_pairs={{0,1},{1,2},{2,3},{3,4},{4,5},{5,6},{6,7},{7,8},{8,9},{9,10},{10,1... | collective-permute-start | bytes 27656 | tf_op jit(solution)/shard_map/ppermute | solution.py:12
  41.5 5.7 %collective-permute-start.4 = (f32[18,128]{1,0:T(8,128)S(1)}, f32[18,128]{1,0:T(8,128)S(1)}, u32[]{:S(2)}, u32[]{:S(2)}) collective-permute-start(f32[18,128]{1,0:T(8,128)S(1)} %bitcast.147), channel_id=1, source_target_pairs={{0,2},{1,3},{2,4},{3,5},{4,6},{5,7},{6,8},{7,9},{8,10},{9,11},{10,... | collective-permute-start | bytes 27656 | tf_op jit(solution)/shard_map/ppermute | solution.py:12
  100.3 11.7 %collective-permute-start.8 = (f32[18,128]{1,0:T(8,128)S(1)}, f32[18,128]{1,0:T(8,128)S(1)}, u32[]{:S(2)}, u32[]{:S(2)}) collective-permute-start(f32[18,128]{1,0:T(8,128)S(1)} %get-tuple-element.17), channel_id=1, source_target_pairs={{2,0},{3,1},{4,2},{5,3},{6,4},{7,5},{8,6},{9,7},{10,8},{11,9},{12,... | collective-permute-start | bytes 27656 | tf_op jit(solution)/shard_map/ppermute | solution.py:12
  101.6 10.4 %collective-permute-start.10 = (f32[18,128]{1,0:T(8,128)S(1)}, f32[18,128]{1,0:T(8,128)S(1)}, u32[]{:S(2)}, u32[]{:S(2)}) collective-permute-start(f32[18,128]{1,0:T(8,128)S(1)} %get-tuple-element.19), channel_id=1, source_target_pairs={{0,1},{1,2},{2,3},{3,4},{4,5},{5,6},{6,7},{7,8},{8,9},{9,10},{10,1... | collective-permute-start | bytes 27656 | tf_op jit(solution)/shard_map/ppermute | solution.py:12
  102.9 9.2 %collective-permute-start.9 = (f32[18,128]{1,0:T(8,128)S(1)}, f32[18,128]{1,0:T(8,128)S(1)}, u32[]{:S(2)}, u32[]{:S(2)}) collective-permute-start(f32[18,128]{1,0:T(8,128)S(1)} %get-tuple-element.20), channel_id=1, source_target_pairs={{1,0},{2,1},{3,2},{4,3},{5,4},{6,5},{7,6},{8,7},{9,8},{10,9},{11,1... | collective-permute-start | bytes 27656 | tf_op jit(solution)/shard_map/ppermute | solution.py:12
  104.2 9.2 %collective-permute-start.11 = (f32[18,128]{1,0:T(8,128)S(1)}, f32[18,128]{1,0:T(8,128)S(1)}, u32[]{:S(2)}, u32[]{:S(2)}) collective-permute-start(f32[18,128]{1,0:T(8,128)S(1)} %get-tuple-element.18), channel_id=1, source_target_pairs={{0,2},{1,3},{2,4},{3,5},{4,6},{5,7},{6,8},{7,9},{8,10},{9,11},{10,... | collective-permute-start | bytes 27656 | tf_op jit(solution)/shard_map/ppermute | solution.py:12
  127.7 11.6 %collective-permute-start.12 = (f32[18,128]{1,0:T(8,128)S(1)}, f32[18,128]{1,0:T(8,128)S(1)}, u32[]{:S(2)}, u32[]{:S(2)}) collective-permute-start(f32[18,128]{1,0:T(8,128)S(1)} %get-tuple-element.13), channel_id=1, source_target_pairs={{0,2},{1,3},{2,4},{3,5},{4,6},{5,7},{6,8},{7,9},{8,10},{9,11},{10,... | collective-permute-start | bytes 27656 | tf_op jit(solution)/shard_map/ppermute | solution.py:12
  133.4 6.8 %collective-permute-start.15 = (f32[18,128]{1,0:T(8,128)S(1)}, f32[18,128]{1,0:T(8,128)S(1)}, u32[]{:S(2)}, u32[]{:S(2)}) collective-permute-start(f32[18,128]{1,0:T(8,128)S(1)} %get-tuple-element.14), channel_id=1, source_target_pairs={{2,0},{3,1},{4,2},{5,3},{6,4},{7,5},{8,6},{9,7},{10,8},{11,9},{12,... | collective-permute-start | bytes 27656 | tf_op jit(solution)/shard_map/ppermute | solution.py:12
  134.7 5.5 %collective-permute-start.14 = (f32[18,128]{1,0:T(8,128)S(1)}, f32[18,128]{1,0:T(8,128)S(1)}, u32[]{:S(2)}, u32[]{:S(2)}) collective-permute-start(f32[18,128]{1,0:T(8,128)S(1)} %get-tuple-element.15), channel_id=1, source_target_pairs={{1,0},{2,1},{3,2},{4,3},{5,4},{6,5},{7,6},{8,7},{9,8},{10,9},{11,1... | collective-permute-start | bytes 27656 | tf_op jit(solution)/shard_map/ppermute | solution.py:12
  136.0 4.2 %collective-permute-start.13 = (f32[18,128]{1,0:T(8,128)S(1)}, f32[18,128]{1,0:T(8,128)S(1)}, u32[]{:S(2)}, u32[]{:S(2)}) collective-permute-start(f32[18,128]{1,0:T(8,128)S(1)} %get-tuple-element.16), channel_id=1, source_target_pairs={{0,1},{1,2},{2,3},{3,4},{4,5},{5,6},{6,7},{7,8},{8,9},{9,10},{10,1... | collective-permute-start | bytes 27656 | tf_op jit(solution)/shard_map/ppermute | solution.py:12
where the time goes:
time: 201 us; the launch traced here: 200 us
  blocking collectives  95.2 us (47%)
  starting transfers between devices  44.4 us (22%)
  other arithmetic  21.3 us (11%)
  matrix products  20.2 us (10%)
  between operations  7.15 us (4%)
  local copies, waits for them, and re-layouts  6.39 us (3%)
  waiting for transfers between devices  5.34 us (3%)
    psum x2, blocking collectives, paired(): lax.psum((jnp.sum(values * values), jnp.sum(values * image_vec)), 'dom')  95.2 us
    ppermute x16, starting transfers between devices, passed_along(): lax.ppermute(value, axis, [(source, source + steps) for source in range(f...  44.4 us
    dot_general x2, matrix products, operate(): lax.dot_general(spread, selector, (((1,), (1,)), ((), ())), precision=lax...  11.2 us
    dot_general x2, matrix products, operate(): jnp.dot(extended, selector, precision=lax.Precision.HIGHEST, preferred_el...  8.99 us
    reduce_sum x2, other arithmetic, operate(): jnp.sum(element_matrix.astype(jnp.float32) * picked[None, :, :], axis=1)  8.08 us
    scatter-add x2, other arithmetic, operate(): summed[:, :own_faces].at[:, send_rows].add(returned.transpose(1, 0, 2))  7.41 us
    ppermute x16, waiting for transfers between devices, passed_along(): lax.ppermute(value, axis, [(source, source + steps) for source in range(f...  5.34 us
  transfers between devices with their start and end apart: 16, of which 4 were waited for; matrix products, arithmetic and copies ran while one was open for 2% of the time, Pallas kernels for 0%

commit v1 on v0

v1 whole, which is shorter than its diff:
```python
import functools
import jax
import jax.numpy as jnp
from jax import lax
from jax.experimental import pallas as pl
from jax.experimental.pallas import tpu as pltpu
from jax.sharding import PartitionSpec as P

LANES = 128
WIDE = 256
MESH = pl.DeviceIdType.MESH
F32 = jnp.float32
BF16 = jnp.bfloat16


def offset_list(block_count):
    half_count = block_count // 2
    return [
        block_index - half_count if block_index < half_count else block_index - half_count + 1
        for block_index in range(block_count)
    ]


def split3(x):
    high = x.astype(BF16)
    rest = x - high.astype(F32)
    middle = rest.astype(BF16)
    low = (rest - middle.astype(F32)).astype(BF16)
    return jnp.concatenate([high, middle, low], axis=0)


def sum3(x):
    rows = x.shape[0] // 3
    return x[:rows] + (x[rows : 2 * rows] + x[2 * rows :])


def dot(a, b):
    return lax.dot_general(a, b, (((1,), (0,)), ((), ())), preferred_element_type=F32)


def dot_nt(a, b):
    return lax.dot_general(a, b, (((1,), (1,)), ((), ())), preferred_element_type=F32)


def kernel(
    cfg,
    rs_ref, em_ref, fm_ref, si_ref, sc_ref, mass_ref, absorb_ref, imp_ref,
    sol_ref, res_ref,
    em_buf, pick_map, send_map, out_buf, ghost_buf, part_buf, ret_buf,
    picked, prod, spread_own, spread_ghost, b_buf, q_buf, sum1, sum2,
    em_sem, fetch_send, fetch_recv, ret_send, ret_recv,
    s1_send, s1_recv, s2_send, s2_recv,
):
    n, g1, g2, trace, sides, elements, own, blocks, width = cfg
    offsets = offset_list(blocks)
    pad = -(-trace // 8) * 8
    own_hi = own // WIDE
    ghost_hi = blocks * width // WIDE
    chunks = sides * elements // WIDE
    per_side = elements // WIDE
    rows_own, rows_ghost = own_hi * pad, ghost_hi * pad
    me = lax.axis_index("dom")
    block_of, in_block = me // g1, lax.rem(me, g1)

    em_copies = [
        pltpu.make_async_copy(
            em_ref.at[pl.ds(s * trace, trace)], em_buf.at[pl.ds(s * trace, trace)], em_sem.at[s]
        )
        for s in range(sides)
    ]
    for copy in em_copies:
        copy.start()

    barrier = pltpu.get_barrier_semaphore()
    waits = jnp.int32((g1 - 1) + (g2 - 1))
    for o in offsets:
        there = me + o
        inside = (there >= 0) & (there < n)
        waits = waits + inside.astype(jnp.int32)

        @pl.when(inside)
        def _():
            pl.semaphore_signal(barrier, inc=1, device_id=(there,), device_id_type=MESH)

    def peer1(d):
        return block_of * g1 + lax.rem(in_block + d, g1)

    def peer2(d):
        return lax.rem(block_of + d, g2) * g1 + in_block

    for d in range(1, g1):
        pl.semaphore_signal(barrier, inc=1, device_id=(peer1(d),), device_id_type=MESH)
    for d in range(1, g2):
        pl.semaphore_signal(barrier, inc=1, device_id=(peer2(d),), device_id_type=MESH)

    lo_iota = lax.broadcasted_iota(jnp.int32, (WIDE, WIDE), 0)
    slot_iota = lax.broadcasted_iota(jnp.int32, (1, width), 1)
    per_wide = WIDE // width
    send_hi = []
    for h in range(ghost_hi):
        cols = []
        for k in range(h * per_wide, (h + 1) * per_wide):
            alive = slot_iota < sc_ref[0:1, k : k + 1]
            cols.append(jnp.where(alive, si_ref[0, k : k + 1, :], -1))
        index = jnp.concatenate(cols, axis=1)
        low = jnp.where(index < 0, -1, index & (WIDE - 1))
        send_map[:, h * WIDE : (h + 1) * WIDE] = (lo_iota == low).astype(F32).astype(BF16)
        send_hi.append(index >> 8)

    def pick_hi(index, stacked, count):
        value = jnp.zeros((pad, WIDE), F32)
        for h in range(count):
            value = jnp.where(index == h, stacked[h * pad : (h + 1) * pad], value)
        return value

    def send_of(split, rnd):
        for h in range(ghost_hi):
            got = sum3(dot(split, send_map[:, h * WIDE : (h + 1) * WIDE]))
            out_buf[rnd, h * pad : (h + 1) * pad, :] = pick_hi(send_hi[h], got, own_hi)

    def piece(ref, rnd, k):
        h, lane = k // per_wide, (k % per_wide) * width
        return ref.at[rnd, pl.ds(h * pad, pad), pl.ds(lane, width)]

    def halo(src, dst, send_sem, recv_sem, rnd, k, step):
        there = me + step
        copy = pltpu.make_async_remote_copy(
            src_ref=piece(src, rnd, k), dst_ref=piece(dst, rnd, k),
            send_sem=send_sem.at[rnd, k], recv_sem=recv_sem.at[rnd, k],
            device_id=(there,), device_id_type=MESH,
        )
        came = me - step
        return copy, (there >= 0) & (there < n), (came >= 0) & (came < n)

    def fetch(rnd, k):
        return halo(out_buf, ghost_buf, fetch_send, fetch_recv, rnd, k, offsets[k])

    def giveback(rnd, k):
        return halo(part_buf, ret_buf, ret_send, ret_recv, rnd, k, -offsets[k])

    def start_all(make, rnd):
        for k in range(blocks):
            copy, to, _ = make(rnd, k)
            pl.when(to)(copy.start)

    def wait_recv_all(make, rnd):
        for k in range(blocks):
            copy, _, came = make(rnd, k)
            pl.when(came)(copy.wait_recv)

    def wait_send_all(make, rnd):
        for k in range(blocks):
            copy, to, _ = make(rnd, k)
            pl.when(to)(copy.wait_send)

    b_buf[...] = jnp.zeros_like(b_buf)
    for h in range(own_hi):
        b_buf[h * pad : h * pad + trace, :] = rs_ref[:, h * WIDE : (h + 1) * WIDE]
    b_split = split3(b_buf[...])
    send_of(b_split, 0)
    for k in range(blocks):
        for rnd in range(2):
            for ref, step in ((ghost_buf, offsets[k]), (ret_buf, -offsets[k])):
                came = me - step

                @pl.when((came < 0) | (came >= n))
                def _():
                    h, lane = k // per_wide, (k % per_wide) * width
                    ref[rnd, h * pad : (h + 1) * pad, lane : lane + width] = jnp.zeros(
                        (pad, width), F32
                    )

    pl.semaphore_wait(barrier, waits)
    start_all(fetch, 0)

    hi_of = []
    for c in range(chunks):
        s, lane = c // per_side, (c % per_side) * WIDE
        index = fm_ref[s : s + 1, lane : lane + WIDE]
        low = index & (WIDE - 1)
        pick_map[:, c * WIDE : (c + 1) * WIDE] = (lo_iota == low).astype(F32).astype(BF16)
        hi_of.append(index >> 8)
    prod[...] = jnp.zeros_like(prod)
    row_live = lax.broadcasted_iota(jnp.int32, (pad, WIDE), 0) < trace
    diag_row = mass_ref[...] + absorb_ref[...].astype(F32) * imp_ref[...]

    def diagonal_times(x):
        return jnp.concatenate(
            [
                x[h * pad : (h + 1) * pad] * diag_row[:, h * WIDE : (h + 1) * WIDE]
                for h in range(own_hi)
            ],
            axis=0,
        )

    def operate(x, split, rnd, before_wait, after_fetch, before_ret):
        for c in range(chunks):
            s, lane = c // per_side, (c % per_side) * WIDE
            got = sum3(dot(split, pick_map[:, c * WIDE : (c + 1) * WIDE]))
            picked[s, :, lane : lane + WIDE] = pick_hi(hi_of[c], got, own_hi)
        before_wait()
        wait_recv_all(fetch, rnd)
        ghost_split = split3(ghost_buf[rnd])
        for c in range(chunks):
            s, lane = c // per_side, (c % per_side) * WIDE
            got = sum3(dot(ghost_split, pick_map[:, c * WIDE : (c + 1) * WIDE]))
            picked[s, :, lane : lane + WIDE] += pick_hi(hi_of[c] - own_hi, got, ghost_hi)
        after_fetch()
        if rnd == 0:
            for copy in em_copies:
                copy.wait()
        for t in range(elements // LANES):
            lanes = slice(t * LANES, (t + 1) * LANES)

            def body(s, acc):
                for c in range(trace):
                    row = picked[s, c : c + 1, lanes]
                    acc = acc + em_buf[s * trace + c, :, lanes].astype(F32) * row
                return acc

            prod[0 : sides * trace, lanes] = lax.fori_loop(
                0, sides, body, jnp.zeros((sides * trace, LANES), F32)
            )

        def spread(c):
            s, lane = c // per_side, (c % per_side) * WIDE
            value = prod[s * trace : s * trace + pad, lane : lane + WIDE]
            return jnp.where(row_live, value, 0.0)

        for c in range(chunks):
            value = spread(c)
            stacked = jnp.concatenate(
                [jnp.where(hi_of[c] == own_hi + h, value, 0.0) for h in range(ghost_hi)], axis=0
            )
            spread_ghost[:, c * WIDE : (c + 1) * WIDE] = split3(stacked)
        part_buf[rnd] = sum3(dot_nt(spread_ghost[...], pick_map[...]))
        start_all(giveback, rnd)
        for c in range(chunks):
            value = spread(c)
            stacked = jnp.concatenate(
                [jnp.where(hi_of[c] == h, value, 0.0) for h in range(own_hi)], axis=0
            )
            spread_own[:, c * WIDE : (c + 1) * WIDE] = split3(stacked)
        result = sum3(dot_nt(spread_own[...], pick_map[...])) + diagonal_times(x)
        before_ret()
        wait_recv_all(giveback, rnd)
        for h in range(ghost_hi):
            value = ret_buf[rnd, h * pad : (h + 1) * pad, :]
            stacked = jnp.concatenate(
                [jnp.where(send_hi[h] == i, value, 0.0) for i in range(own_hi)], axis=0
            )
            result = result + sum3(
                dot_nt(split3(stacked), send_map[:, h * WIDE : (h + 1) * WIDE])
            )
        return result

    def stage1(rnd, d):
        slot = sum1.at[rnd, in_block]
        return pltpu.make_async_remote_copy(
            src_ref=slot, dst_ref=slot, send_sem=s1_send.at[rnd, d], recv_sem=s1_recv.at[rnd, d],
            device_id=(peer1(d),), device_id_type=MESH,
        )

    def stage2(rnd, d):
        slot = sum2.at[rnd, block_of]
        return pltpu.make_async_remote_copy(
            src_ref=slot, dst_ref=slot, send_sem=s2_send.at[rnd, d], recv_sem=s2_recv.at[rnd, d],
            device_id=(peer2(d),), device_id_type=MESH,
        )

    def lane_sums(x):
        total = jnp.sum(x, axis=0, keepdims=True)
        return total[:, :LANES] + total[:, LANES:]

    def begin_sum(rnd, x, y):
        sum1[rnd, in_block] = jnp.concatenate([lane_sums(x), lane_sums(y)], axis=0)
        for d in range(1, g1):
            stage1(rnd, d).start()

    def middle_sum(rnd):
        for d in range(1, g1):
            stage1(rnd, d).wait_recv()
        sum2[rnd, block_of] = jnp.sum(sum1[rnd], axis=0)
        for d in range(1, g2):
            stage2(rnd, d).start()

    def end_sum(rnd):
        for d in range(1, g2):
            stage2(rnd, d).wait_recv()
        total = jnp.sum(jnp.sum(sum2[rnd], axis=0), axis=1, keepdims=True)
        return total[0:1], total[1:2]

    nothing = lambda: None
    q = operate(b_buf[...], b_split, 0, nothing, nothing, nothing)
    q_buf[...] = q
    q_split = split3(q)
    send_of(q_split, 1)
    start_all(fetch, 1)
    b = b_buf[...]
    begin_sum(0, b * b, b * q)
    w = operate(q_buf[...], q_split, 1, nothing, lambda: middle_sum(0), nothing)
    rr, curve = end_sum(0)
    step0 = rr / curve
    b, q = b_buf[...], q_buf[...]
    r1 = b - step0 * q
    z1 = q - step0 * w
    begin_sum(1, r1 * r1, r1 * z1)
    middle_sum(1)
    new, curve = end_sum(1)
    beta = new / rr
    step1 = new / (curve - beta * new / step0)
    sol = step0 * b + step1 * (r1 + beta * b)
    res = r1 - step1 * (z1 + beta * q)
    for h in range(own_hi):
        sol_ref[:, h * WIDE : (h + 1) * WIDE] = sol[h * pad : h * pad + trace]
        res_ref[:, h * WIDE : (h + 1) * WIDE] = res[h * pad : h * pad + trace]
    for rnd in range(2):
        wait_send_all(fetch, rnd)
        wait_send_all(giveback, rnd)
        for d in range(1, g1):
            stage1(rnd, d).wait_send()
        for d in range(1, g2):
            stage2(rnd, d).wait_send()


def solution(mesh):
    n = mesh.shape["dom"]
    g1 = next(g for g in range(1, n + 1) if n % g == 0 and g * g >= n)
    g2 = n // g1

    def shards(rs, em, fm, si, sc, mass, absorb, imp):
        trace, own = rs.shape
        sides, elements = fm.shape
        blocks, width = si.shape[1:]
        pad = -(-trace // 8) * 8
        rows_own = own // WIDE * pad
        rows_ghost = blocks * width // WIDE * pad
        picks = sides * elements
        dofs = sides * trace
        cfg = (n, g1, g2, trace, sides, elements, own, blocks, width)
        dma = pltpu.SemaphoreType.DMA
        vmem = pl.BlockSpec(memory_space=pltpu.VMEM)
        return pl.pallas_call(
            functools.partial(kernel, cfg),
            out_shape=[jax.ShapeDtypeStruct(rs.shape, F32)] * 2,
            in_specs=[vmem, pl.BlockSpec(memory_space=pl.ANY)] + [vmem] * 6,
            out_specs=[vmem] * 2,
            scratch_shapes=[
                pltpu.VMEM((dofs, dofs, elements), BF16),
                pltpu.VMEM((WIDE, picks), BF16),
                pltpu.VMEM((WIDE, blocks * width), BF16),
                pltpu.VMEM((2, rows_ghost, WIDE), F32),
                pltpu.VMEM((2, rows_ghost, WIDE), F32),
                pltpu.VMEM((2, rows_ghost, WIDE), F32),
                pltpu.VMEM((2, rows_ghost, WIDE), F32),
                pltpu.VMEM((sides, pad, elements), F32),
                pltpu.VMEM((dofs + 8, elements), F32),
                pltpu.VMEM((3 * rows_own, picks), BF16),
                pltpu.VMEM((3 * rows_ghost, picks), BF16),
                pltpu.VMEM((rows_own, WIDE), F32),
                pltpu.VMEM((rows_own, WIDE), F32),
                pltpu.VMEM((2, g1, 2, LANES), F32),
                pltpu.VMEM((2, g2, 2, LANES), F32),
                dma((sides,)),
                dma((2, blocks)), dma((2, blocks)), dma((2, blocks)), dma((2, blocks)),
                dma((2, g1)), dma((2, g1)), dma((2, g2)), dma((2, g2)),
            ],
            compiler_params=pltpu.CompilerParams(
                collective_id=0, has_side_effects=True, vmem_limit_bytes=62 * 1024 * 1024
            ),
        )(rs, em, fm, si, sc, mass.reshape(1, own), absorb.reshape(1, own), imp.reshape(1, own))

    placed = (
        P(None, "dom"),
        P(None, None, "dom"),
        P(None, "dom"),
        P("dom", None, None),
        P("dom", None),
        P("dom"),
        P("dom"),
        P("dom"),
    )
    return jax.shard_map(
        shards,
        mesh=mesh,
        in_specs=placed,
        out_specs=(P(None, "dom"), P(None, "dom")),
        check_vma=False,
    )
```

time: 201 us -> 38 us (0.19)
  blocking collectives: 95.2 us -> 0 us
  starting transfers between devices: 44.4 us -> 0 us
  Pallas kernels: 0 us -> 34 us
  other arithmetic: 21.3 us -> 0 us
  matrix products: 20.2 us -> 0 us
  between operations: 7.15 us -> 0.64 us
  waiting for transfers between devices: 5.34 us -> 0 us
  local copies, waits for them, and re-layouts: 6.39 us -> 3.08 us
    psum x2 -> x0, blocking collectives: 95.2 us -> none  [paired(): lax.psum((jnp.sum(values * values), jnp.sum(values * image_vec)), 'dom')]
    ppermute x16 -> x0, starting transfers between devices: 44.4 us -> none  [passed_along(): lax.ppermute(value, axis, [(source, source + steps) for source in range(f...]
    pallas_call x0 -> x1, Pallas kernels: none -> 34 us  [shards(): pl.pallas_call(functools.partial(kernel, cfg), out_shape=[jax.ShapeDtypeS...]
    dot_general x4 -> x0, matrix products: 20.2 us -> none  [the longest x2 11.2 us: operate(): lax.dot_general(spread, selector, (((1,), (1,)), ((), ())), precision=lax...]
    reduce_sum x5 -> x0, other arithmetic: 10.2 us -> none  [the longest x2 8.08 us: operate(): jnp.sum(element_matrix.astype(jnp.float32) * picked[None, :, :], axis=1)]
    scatter-add x2 -> x0, other arithmetic: 7.41 us -> none  [operate(): summed[:, :own_faces].at[:, send_rows].add(returned.transpose(1, 0, 2))]
    ppermute x16 -> x0, waiting for transfers between devices: 5.34 us -> none  [passed_along(): lax.ppermute(value, axis, [(source, source + steps) for source in range(f...]
    gather x4 -> x0, local copies, waits for them, and re-layouts: 2.3 us -> none  [operate(): jnp.take(field_now, send_rows, axis=1).transpose(1, 0, 2)]
  transfers between devices with their start and end apart: 16 -> 0, of which waited for: 4 -> 0; matrix products, arithmetic and copies ran while one was open for 2% -> 0% of each run, Pallas kernels for 0% -> 0%
where the time goes in v1:
time: 38 us; the launch traced here: 37.8 us
  Pallas kernels  34 us (89%)
  local copies, waits for them, and re-layouts  3.08 us (8%)
  between operations  0.64 us (2%)
    pallas_call x1, Pallas kernels, shards(): pl.pallas_call(functools.partial(kernel, cfg), out_shape=[jax.ShapeDtypeS...  34 us
    unnamed x2, local copies, waits for them, and re-layouts  3.08 us

profile of v1, /device:TPU:0, one launch (start us, length us, event | category | flops | bytes accessed | tf_op | source)
XLA Modules:
  0.0 37.8 jit_solution(18122969263011312101)
XLA Ops:
  0.6 34.0 %shard_map.95 = (f32[18,1024]{1,0:T(8,128)}, f32[18,1024]{1,0:T(8,128)}) custom-call(f32[18,1024]{1,0:T(8,128)} %rs_ref.1, bf16[72,72,512]{2,1,0:T(8,128)(2,1)} %em_ref.1, s32[4,512]{1,0:T(4,128)} %fm_ref.1, s32[1,4,128]{2,1,0:T(4,128)} %si_ref.1, s32[1,4]{1,0:T(1,128)} %sc_ref.1, f32[1,1024]{1,0:T(1,128)} %bitcast.3, s32[1,1024]{1,0:T(1,128)} %bitcast.4, ...), custom_call_target="tpu_custom_call" | custom-call | tf_op jit(solution)/shard_map/pallas_call | solution.py:343
  34.7 1.5 %copy.12 = f32[18,1024]{1,0:T(8,128)} copy(f32[18,1024]{1,0:T(8,128)} %get-tuple-element.4) | data formatting | bytes 147456
  36.2 1.5 %copy.13 = f32[18,1024]{1,0:T(8,128)} copy(f32[18,1024]{1,0:T(8,128)} %get-tuple-element.5) | data formatting | bytes 147456

commit v2 on v1

--- a/solution.py
+++ b/solution.py
@@ -44,12 +44,13 @@
 
 def kernel(
     cfg,
-    rs_ref, em_ref, fm_ref, si_ref, sc_ref, mass_ref, absorb_ref, imp_ref,
+    rs_in, em_ref, fm_in, si_in, sc_in, mass_in, absorb_in, imp_in,
     sol_ref, res_ref,
+    rs_ref, fm_ref, si_ref, sc_ref, mass_ref, absorb_ref, imp_ref,
     em_buf, pick_map, send_map, out_buf, ghost_buf, part_buf, ret_buf,
-    picked, prod, spread_own, spread_ghost, b_buf, q_buf, sum1, sum2,
-    em_sem, fetch_send, fetch_recv, ret_send, ret_recv,
-    s1_send, s1_recv, s2_send, s2_recv,
+    picked, prod, spread_own, spread_ghost, b_buf, q_buf, sum1, sum2, sum_all,
+    in_sem, em_sem, fetch_send, fetch_recv, ret_send, ret_recv,
+    s1_send, s1_recv, s2_send, s2_recv, all_send, all_recv,
 ):
     n, g1, g2, trace, sides, elements, own, blocks, width = cfg
     offsets = offset_list(blocks)
@@ -62,15 +63,6 @@
     me = lax.axis_index("dom")
     block_of, in_block = me // g1, lax.rem(me, g1)
 
-    em_copies = [
-        pltpu.make_async_copy(
-            em_ref.at[pl.ds(s * trace, trace)], em_buf.at[pl.ds(s * trace, trace)], em_sem.at[s]
-        )
-        for s in range(sides)
-    ]
-    for copy in em_copies:
-        copy.start()
-
     barrier = pltpu.get_barrier_semaphore()
     waits = jnp.int32((g1 - 1) + (g2 - 1))
     for o in offsets:
@@ -93,6 +85,28 @@
     for d in range(1, g2):
         pl.semaphore_signal(barrier, inc=1, device_id=(peer2(d),), device_id_type=MESH)
 
+    in_copies = [
+        pltpu.make_async_copy(source, target, in_sem.at[i])
+        for i, (source, target) in enumerate(
+            (
+                (rs_in, rs_ref), (si_in, si_ref), (sc_in, sc_ref), (fm_in, fm_ref),
+                (mass_in, mass_ref), (absorb_in, absorb_ref), (imp_in, imp_ref),
+            )
+        )
+    ]
+    for copy in in_copies:
+        copy.start()
+    em_copies = [
+        pltpu.make_async_copy(
+            em_ref.at[pl.ds(s * trace, trace)], em_buf.at[pl.ds(s * trace, trace)], em_sem.at[s]
+        )
+        for s in range(sides)
+    ]
+    for copy in em_copies:
+        copy.start()
+
+    for copy in in_copies[:3]:
+        copy.wait()
     lo_iota = lax.broadcasted_iota(jnp.int32, (WIDE, WIDE), 0)
     slot_iota = lax.broadcasted_iota(jnp.int32, (1, width), 1)
     per_wide = WIDE // width
@@ -173,6 +187,8 @@
     pl.semaphore_wait(barrier, waits)
     start_all(fetch, 0)
 
+    for copy in in_copies[3:]:
+        copy.wait()
     hi_of = []
     for c in range(chunks):
         s, lane = c // per_side, (c % per_side) * WIDE
@@ -193,19 +209,17 @@
             axis=0,
         )
 
-    def operate(x, split, rnd, before_wait, after_fetch, before_ret):
+    def operate(x, split, rnd, after_product):
         for c in range(chunks):
             s, lane = c // per_side, (c % per_side) * WIDE
             got = sum3(dot(split, pick_map[:, c * WIDE : (c + 1) * WIDE]))
             picked[s, :, lane : lane + WIDE] = pick_hi(hi_of[c], got, own_hi)
-        before_wait()
         wait_recv_all(fetch, rnd)
         ghost_split = split3(ghost_buf[rnd])
         for c in range(chunks):
             s, lane = c // per_side, (c % per_side) * WIDE
             got = sum3(dot(ghost_split, pick_map[:, c * WIDE : (c + 1) * WIDE]))
             picked[s, :, lane : lane + WIDE] += pick_hi(hi_of[c] - own_hi, got, ghost_hi)
-        after_fetch()
         if rnd == 0:
             for copy in em_copies:
                 copy.wait()
@@ -227,6 +241,7 @@
             value = prod[s * trace : s * trace + pad, lane : lane + WIDE]
             return jnp.where(row_live, value, 0.0)
 
+        after_product()
         for c in range(chunks):
             value = spread(c)
             stacked = jnp.concatenate(
@@ -242,7 +257,6 @@
             )
             spread_own[:, c * WIDE : (c + 1) * WIDE] = split3(stacked)
         result = sum3(dot_nt(spread_own[...], pick_map[...])) + diagonal_times(x)
-        before_ret()
         wait_recv_all(giveback, rnd)
         for h in range(ghost_hi):
             value = ret_buf[rnd, h * pad : (h + 1) * pad, :]
@@ -254,17 +268,17 @@
             )
         return result
 
-    def stage1(rnd, d):
-        slot = sum1.at[rnd, in_block]
+    def stage1(d):
+        slot = sum1.at[in_block]
         return pltpu.make_async_remote_copy(
-            src_ref=slot, dst_ref=slot, send_sem=s1_send.at[rnd, d], recv_sem=s1_recv.at[rnd, d],
+            src_ref=slot, dst_ref=slot, send_sem=s1_send.at[d], recv_sem=s1_recv.at[d],
             device_id=(peer1(d),), device_id_type=MESH,
         )
 
-    def stage2(rnd, d):
-        slot = sum2.at[rnd, block_of]
+    def stage2(d):
+        slot = sum2.at[block_of]
         return pltpu.make_async_remote_copy(
-            src_ref=slot, dst_ref=slot, send_sem=s2_send.at[rnd, d], recv_sem=s2_recv.at[rnd, d],
+            src_ref=slot, dst_ref=slot, send_sem=s2_send.at[d], recv_sem=s2_recv.at[d],
             device_id=(peer2(d),), device_id_type=MESH,
         )
 
@@ -272,41 +286,59 @@
         total = jnp.sum(x, axis=0, keepdims=True)
         return total[:, :LANES] + total[:, LANES:]
 
-    def begin_sum(rnd, x, y):
-        sum1[rnd, in_block] = jnp.concatenate([lane_sums(x), lane_sums(y)], axis=0)
+    def pair_of(x, y):
+        return jnp.concatenate([lane_sums(x), lane_sums(y)], axis=0)
+
+    def begin_sum(x, y):
+        sum1[in_block] = pair_of(x, y)
         for d in range(1, g1):
-            stage1(rnd, d).start()
-
-    def middle_sum(rnd):
+            stage1(d).start()
+
+    def middle_sum():
         for d in range(1, g1):
-            stage1(rnd, d).wait_recv()
-        sum2[rnd, block_of] = jnp.sum(sum1[rnd], axis=0)
+            stage1(d).wait_recv()
+        sum2[block_of] = jnp.sum(sum1[...], axis=0)
         for d in range(1, g2):
-            stage2(rnd, d).start()
-
-    def end_sum(rnd):
+            stage2(d).start()
+
+    def totals(parts):
+        total = jnp.sum(jnp.sum(parts, axis=0), axis=1, keepdims=True)
+        return total[0:1], total[1:2]
+
+    def end_sum():
         for d in range(1, g2):
-            stage2(rnd, d).wait_recv()
-        total = jnp.sum(jnp.sum(sum2[rnd], axis=0), axis=1, keepdims=True)
-        return total[0:1], total[1:2]
-
-    nothing = lambda: None
-    q = operate(b_buf[...], b_split, 0, nothing, nothing, nothing)
+            stage2(d).wait_recv()
+        return totals(sum2[...])
+
+    def straight(d):
+        return pltpu.make_async_remote_copy(
+            src_ref=sum_all.at[0], dst_ref=sum_all.at[d],
+            send_sem=all_send.at[d], recv_sem=all_recv.at[d],
+            device_id=(lax.rem(me + d, n),), device_id_type=MESH,
+        )
+
+    def sum_straight(x, y):
+        sum_all[0] = pair_of(x, y)
+        for d in range(1, n):
+            straight(d).start()
+        for d in range(1, n):
+            straight(d).wait_recv()
+        return totals(sum_all[...])
+
+    q = operate(b_buf[...], b_split, 0, lambda: None)
     q_buf[...] = q
     q_split = split3(q)
     send_of(q_split, 1)
     start_all(fetch, 1)
     b = b_buf[...]
-    begin_sum(0, b * b, b * q)
-    w = operate(q_buf[...], q_split, 1, nothing, lambda: middle_sum(0), nothing)
-    rr, curve = end_sum(0)
+    begin_sum(b * b, b * q)
+    w = operate(q_buf[...], q_split, 1, middle_sum)
+    rr, curve = end_sum()
     step0 = rr / curve
     b, q = b_buf[...], q_buf[...]
     r1 = b - step0 * q
     z1 = q - step0 * w
-    begin_sum(1, r1 * r1, r1 * z1)
-    middle_sum(1)
-    new, curve = end_sum(1)
+    new, curve = sum_straight(r1 * r1, r1 * z1)
     beta = new / rr
     step1 = new / (curve - beta * new / step0)
     sol = step0 * b + step1 * (r1 + beta * b)
@@ -317,10 +349,23 @@
     for rnd in range(2):
         wait_send_all(fetch, rnd)
         wait_send_all(giveback, rnd)
-        for d in range(1, g1):
-            stage1(rnd, d).wait_send()
-        for d in range(1, g2):
-            stage2(rnd, d).wait_send()
+    for d in range(1, g1):
+        stage1(d).wait_send()
+    for d in range(1, g2):
+        stage2(d).wait_send()
+    for d in range(1, n):
+        straight(d).wait_send()
+
+
+def put_out(sol_ref, res_ref, sol_out, res_out, sems):
+    copies = [
+        pltpu.make_async_copy(sol_ref, sol_out, sems.at[0]),
+        pltpu.make_async_copy(res_ref, res_out, sems.at[1]),
+    ]
+    for copy in copies:
+        copy.start()
+    for copy in copies:
+        copy.wait()
 
 
 def solution(mesh):
@@ -340,12 +385,19 @@
         cfg = (n, g1, g2, trace, sides, elements, own, blocks, width)
         dma = pltpu.SemaphoreType.DMA
         vmem = pl.BlockSpec(memory_space=pltpu.VMEM)
-        return pl.pallas_call(
+        sol, res = pl.pallas_call(
             functools.partial(kernel, cfg),
-            out_shape=[jax.ShapeDtypeStruct(rs.shape, F32)] * 2,
-            in_specs=[vmem, pl.BlockSpec(memory_space=pl.ANY)] + [vmem] * 6,
+            out_shape=[pltpu.VMEM(rs.shape, F32)] * 2,
+            in_specs=[pl.BlockSpec(memory_space=pltpu.HBM)] * 8,
             out_specs=[vmem] * 2,
             scratch_shapes=[
+                pltpu.VMEM(rs.shape, F32),
+                pltpu.VMEM(fm.shape, jnp.int32),
+                pltpu.VMEM(si.shape, jnp.int32),
+                pltpu.VMEM(sc.shape, jnp.int32),
+                pltpu.VMEM((1, own), F32),
+                pltpu.VMEM((1, own), jnp.int32),
+                pltpu.VMEM((1, own), F32),
                 pltpu.VMEM((dofs, dofs, elements), BF16),
                 pltpu.VMEM((WIDE, picks), BF16),
                 pltpu.VMEM((WIDE, blocks * width), BF16),
@@ -359,16 +411,25 @@
                 pltpu.VMEM((3 * rows_ghost, picks), BF16),
                 pltpu.VMEM((rows_own, WIDE), F32),
                 pltpu.VMEM((rows_own, WIDE), F32),
-                pltpu.VMEM((2, g1, 2, LANES), F32),
-                pltpu.VMEM((2, g2, 2, LANES), F32),
-                dma((sides,)),
+                pltpu.VMEM((g1, 2, LANES), F32),
+                pltpu.VMEM((g2, 2, LANES), F32),
+                pltpu.VMEM((n, 2, LANES), F32),
+                dma((7,)), dma((sides,)),
                 dma((2, blocks)), dma((2, blocks)), dma((2, blocks)), dma((2, blocks)),
-                dma((2, g1)), dma((2, g1)), dma((2, g2)), dma((2, g2)),
+                dma((g1,)), dma((g1,)), dma((g2,)), dma((g2,)), dma((n,)), dma((n,)),
             ],
             compiler_params=pltpu.CompilerParams(
                 collective_id=0, has_side_effects=True, vmem_limit_bytes=62 * 1024 * 1024
             ),
         )(rs, em, fm, si, sc, mass.reshape(1, own), absorb.reshape(1, own), imp.reshape(1, own))
+        return pl.pallas_call(
+            put_out,
+            out_shape=[jax.ShapeDtypeStruct(rs.shape, F32)] * 2,
+            in_specs=[vmem] * 2,
+            out_specs=[pl.BlockSpec(memory_space=pltpu.HBM)] * 2,
+            scratch_shapes=[dma((2,))],
+            compiler_params=pltpu.CompilerParams(vmem_limit_bytes=8 * 1024 * 1024),
+        )(sol, res)
 
     placed = (
         P(None, "dom"),

time: 38 us -> 32.4 us (0.85)
  local copies, waits for them, and re-layouts: 3.08 us -> 0 us
  Pallas kernels: 34 us -> 31.6 us
    unnamed x2 -> x0, local copies, waits for them, and re-layouts: 3.08 us -> none
    pallas_call x1 -> x2, Pallas kernels: 34 us -> 31.6 us  [the longest x1 30.9 us: shards(): pl.pallas_call(functools.partial(kernel, cfg), out_shape=[pltpu.VMEM(rs.s...]
where the time goes in v2:
time: 32.4 us; the launch traced here: 32.2 us
  Pallas kernels  31.6 us (98%)
  between operations  0.64 us (2%)
    pallas_call x1, Pallas kernels, shards(): pl.pallas_call(functools.partial(kernel, cfg), out_shape=[pltpu.VMEM(rs.s...  30.9 us
    pallas_call x1, Pallas kernels, shards(): pl.pallas_call(put_out, out_shape=[jax.ShapeDtypeStruct(rs.shape, F32)] *...  0.69 us

profile of v2, /device:TPU:0, one launch (start us, length us, event | category | flops | bytes accessed | tf_op | source)
XLA Modules:
  0.0 32.2 jit_solution(3095541759985102778)
XLA Ops:
  0.6 30.9 %shard_map.95 = (f32[18,1024]{1,0:T(8,128)S(1)}, f32[18,1024]{1,0:T(8,128)S(1)}) custom-call(f32[18,1024]{1,0:T(8,128)} %rs_in.1, bf16[72,72,512]{2,1,0:T(8,128)(2,1)} %em_ref.1, s32[4,512]{1,0:T(4,128)} %fm_in.1, s32[1,4,128]{2,1,0:T(4,128)} %si_in.1, s32[1,4]{1,0:T(1,128)} %sc_in.1, f32[1,1024]{1,0:T(1,128)} %bitcast.3, s32[1,1024]{1,0:T(1,128)} %bitcast.4, ...), custom_call_target="tpu_custom_call" | custom-call | tf_op jit(solution)/shard_map/pallas_call | solution.py:388
  31.5 0.7 %shard_map.96 = (f32[18,1024]{1,0:T(8,128)}, f32[18,1024]{1,0:T(8,128)}) custom-call(f32[18,1024]{1,0:T(8,128)S(1)} %get-tuple-element.4.sol_ref, f32[18,1024]{1,0:T(8,128)S(1)} %get-tuple-element.5.res_ref), custom_call_target="tpu_custom_call" | custom-call | tf_op jit(solution)/shard_map/pallas_call | solution.py:425

commit v3 on v2

--- a/solution.py
+++ b/solution.py
@@ -152,8 +152,10 @@
     def giveback(rnd, k):
         return halo(part_buf, ret_buf, ret_send, ret_recv, rnd, k, -offsets[k])
 
+    far_first = sorted(range(blocks), key=lambda k: -abs(offsets[k]))
+
     def start_all(make, rnd):
-        for k in range(blocks):
+        for k in far_first:
             copy, to, _ = make(rnd, k)
             pl.when(to)(copy.start)
 
@@ -258,14 +260,14 @@
             spread_own[:, c * WIDE : (c + 1) * WIDE] = split3(stacked)
         result = sum3(dot_nt(spread_own[...], pick_map[...])) + diagonal_times(x)
         wait_recv_all(giveback, rnd)
+        came_back = []
         for h in range(ghost_hi):
             value = ret_buf[rnd, h * pad : (h + 1) * pad, :]
             stacked = jnp.concatenate(
                 [jnp.where(send_hi[h] == i, value, 0.0) for i in range(own_hi)], axis=0
             )
-            result = result + sum3(
-                dot_nt(split3(stacked), send_map[:, h * WIDE : (h + 1) * WIDE])
-            )
+            came_back.append(split3(stacked))
+        result = result + sum3(dot_nt(jnp.concatenate(came_back, axis=1), send_map[...]))
         return result
 
     def stage1(d):
@@ -319,7 +321,7 @@
 
     def sum_straight(x, y):
         sum_all[0] = pair_of(x, y)
-        for d in range(1, n):
+        for d in sorted(range(1, n), key=lambda d: abs(2 * d - n)):
             straight(d).start()
         for d in range(1, n):
             straight(d).wait_recv()

time: 32.4 us -> 32.2 us (level)
  no operation moved by 1% of the time
where the time goes in v3:
time: 32.2 us; the launch traced here: 32.1 us
  Pallas kernels  31.4 us (98%)
  between operations  0.64 us (2%)
    pallas_call x1, Pallas kernels, shards(): pl.pallas_call(functools.partial(kernel, cfg), out_shape=[pltpu.VMEM(rs.s...  30.8 us
    pallas_call x1, Pallas kernels, shards(): pl.pallas_call(put_out, out_shape=[jax.ShapeDtypeStruct(rs.shape, F32)] *...  0.69 us

profile of v3, /device:TPU:0, one launch (start us, length us, event | category | flops | bytes accessed | tf_op | source)
XLA Modules:
  0.0 32.1 jit_solution(11661342434152883665)
XLA Ops:
  0.6 30.8 %shard_map.95 = (f32[18,1024]{1,0:T(8,128)S(1)}, f32[18,1024]{1,0:T(8,128)S(1)}) custom-call(f32[18,1024]{1,0:T(8,128)} %rs_in.1, bf16[72,72,512]{2,1,0:T(8,128)(2,1)} %em_ref.1, s32[4,512]{1,0:T(4,128)} %fm_in.1, s32[1,4,128]{2,1,0:T(4,128)} %si_in.1, s32[1,4]{1,0:T(1,128)} %sc_in.1, f32[1,1024]{1,0:T(1,128)} %bitcast.3, s32[1,1024]{1,0:T(1,128)} %bitcast.4, ...), custom_call_target="tpu_custom_call" | custom-call | tf_op jit(solution)/shard_map/pallas_call | solution.py:390
  31.4 0.7 %shard_map.96 = (f32[18,1024]{1,0:T(8,128)}, f32[18,1024]{1,0:T(8,128)}) custom-call(f32[18,1024]{1,0:T(8,128)S(1)} %get-tuple-element.4.sol_ref, f32[18,1024]{1,0:T(8,128)S(1)} %get-tuple-element.5.res_ref), custom_call_target="tpu_custom_call" | custom-call | tf_op jit(solution)/shard_map/pallas_call | solution.py:427
